TPU v7x, 32 devices: a whole 2x2x4 slice. The times are simulated.
32 devices in a mesh: view: 8 (over z, y), tok: 2 (over x), obj: 2 (over core).
Axes of the slice: x: 2, y: 2, z: 4, core: 2. Of those that a mesh axis runs over, the one named last changes fastest.
Arguments:
- latents: bfloat16 [512, 8, 2, 1280], P('tok', 'view', 'obj'), parts along dimension 2, may hold values from -8 to 8
- query_weight: bfloat16 [1280, 1024], P(None, 'tok'), may hold values from -2 to 2
- key_weight: bfloat16 [1280, 1024], P(None, 'tok'), may hold values from -14 to 14
- value_weight: bfloat16 [1280, 1024], P(None, 'tok'), may hold values from -0.15625 to 0.15625
- output_weight: bfloat16 [1024, 1280], P('tok'), may hold values from -0.1875 to 0.1875
- value_units: bfloat16 [1280, 5120], P(None, 'tok'), may hold values from -0.15625 to 0.15625
- gate_units: bfloat16 [1280, 5120], P(None, 'tok'), may hold values from -0.15625 to 0.15625
- down_weight: bfloat16 [5120, 1280], P('tok'), may hold values from -0.078125 to 0.078125
Outputs:
- refined: bfloat16 [512, 8, 2, 1280], P('tok', 'view', 'obj'), parts along dimension 2
There are 2 independent parts, one for each index of `obj`. A program takes and returns all parts, laid end to end along the dimension named above; an argument that names none is the same for every part. Nothing has to cross between parts.
All inputs are finite; a program needn't handle non-finite values.
Results may differ from a plain program's by a relative error of at most 0.012.
Values may be sent and summed in bfloat16 or wider, within the bound.
A program may use at most 128 MiB of HBM per device.

v0:
```python
import functools

import jax
import jax.numpy as jnp
from jax import lax
from jax.experimental import pallas as pl
from jax.experimental.pallas import tpu as pltpu
from jax.sharding import PartitionSpec as P

HS = 64
MESH = pl.DeviceIdType.MESH
VMEM = pl.BlockSpec(memory_space=pltpu.VMEM)
ANY = pl.BlockSpec(memory_space=pl.ANY)


epsilon = 1e-05


def passed_along(block, axis, distance):
    devices = range(lax.axis_size(axis))
    route = [((i - distance) % len(devices), i) for i in devices]
    return lax.ppermute(block, axis, route)


def normalize(stream):
    average = jnp.mean(stream, -1, keepdims=True)
    centered = stream - average
    spread = jnp.mean(centered * centered, -1, keepdims=True)
    return centered * lax.rsqrt(spread + epsilon)


def meet(axes):
    barrier = pltpu.get_barrier_semaphore()
    for peer in axes:
        pl.semaphore_signal(barrier, inc=1, device_id=peer, device_id_type=MESH)
    pl.semaphore_wait(barrier, len(axes))


def peers_of(axis, count):
    me = lax.axis_index(axis)
    return [lax.rem(me + d, count) for d in range(1, count)]


def post(sources, results, axis, count, send_sem, recv_sem, own_sem, scattered):
    me = lax.axis_index(axis)
    waits = []
    for number, (source, result) in enumerate(zip(sources, results)):
        for d in range(1, count):
            peer = lax.rem(me + d, count)
            sender = lax.rem(me - d + count, count)
            copy = pltpu.make_async_remote_copy(
                src_ref=source.at[peer] if scattered else source,
                dst_ref=result.at[me],
                send_sem=send_sem.at[number, d],
                recv_sem=recv_sem.at[number, d],
                device_id={axis: peer},
                device_id_type=MESH,
            )
            arrival = pltpu.make_async_remote_copy(
                src_ref=source.at[peer] if scattered else source,
                dst_ref=result.at[sender],
                send_sem=send_sem.at[number, d],
                recv_sem=recv_sem.at[number, d],
                device_id={axis: peer},
                device_id_type=MESH,
            )
            copy.start()
            waits.append(copy.wait_send)
            waits.append(arrival.wait_recv)
        own = pltpu.make_async_copy(
            source.at[me] if scattered else source, result.at[me], own_sem.at[number]
        )
        own.start()
        waits.append(own.wait)
    return waits


def token_kernel(count, scattered, x_ref, out_ref, send_sem, recv_sem, own_sem):
    meet([{"tok": p} for p in peers_of("tok", count)])
    for wait in post([x_ref], [out_ref], "tok", count, send_sem, recv_sem, own_sem, scattered):
        wait()


def over_tokens(x, count, scattered, number):
    block = x.shape[1:] if scattered else x.shape
    return pl.pallas_call(
        functools.partial(token_kernel, count, scattered),
        out_shape=jax.ShapeDtypeStruct((count,) + block, x.dtype),
        in_specs=[VMEM],
        out_specs=ANY,
        scratch_shapes=[
            pltpu.SemaphoreType.DMA((1, count)),
            pltpu.SemaphoreType.DMA((1, count)),
            pltpu.SemaphoreType.DMA((1,)),
        ],
        compiler_params=pltpu.CompilerParams(collective_id=number, has_side_effects=True),
        name=f"over_tokens_{number}",
    )(x)


def heads_kernel(views, toks, q, k, v, w, q_out, k_out, v_out, w_out, *sems):
    meet(
        [{"view": p} for p in peers_of("view", views)]
        + [{"tok": p} for p in peers_of("tok", toks)]
    )
    waits = post([q, k, v], [q_out, k_out, v_out], "view", views, *sems[:3], True)
    waits += post([w], [w_out], "tok", toks, *sems[3:], False)
    for wait in waits:
        wait()


def spread_heads(queries, keys, values, weight, views, toks):
    like = jax.ShapeDtypeStruct(queries.shape, queries.dtype)
    return pl.pallas_call(
        functools.partial(heads_kernel, views, toks),
        out_shape=(like, like, like, jax.ShapeDtypeStruct((toks,) + weight.shape, weight.dtype)),
        in_specs=[VMEM] * 4,
        out_specs=(ANY,) * 4,
        scratch_shapes=[
            pltpu.SemaphoreType.DMA((3, views)),
            pltpu.SemaphoreType.DMA((3, views)),
            pltpu.SemaphoreType.DMA((3,)),
            pltpu.SemaphoreType.DMA((1, toks)),
            pltpu.SemaphoreType.DMA((1, toks)),
            pltpu.SemaphoreType.DMA((1,)),
        ],
        compiler_params=pltpu.CompilerParams(collective_id=1, has_side_effects=True),
        name="spread_heads",
    )(queries, keys, values, weight)


def attention_kernel(
    views, toks, q_ref, k_ref, v_ref, out_ref, keys, scores, staged, send_sem, recv_sem, own_sem
):
    view, tok = lax.axis_index("view"), lax.axis_index("tok")
    others = [
        (dv, dt) for dv in range(views) for dt in range(toks) if dv or dt
    ]
    meet(
        [
            {"view": lax.rem(view + dv, views), "tok": lax.rem(tok + dt, toks)}
            for dv, dt in others
        ]
    )
    rows = staged.shape[-1]
    length = k_ref.shape[-1]
    for block in range(views):
        keys[block] = k_ref[block].T

    def attend(target):
        q = q_ref[target]
        highest = jnp.full((1, length), -1e30, jnp.float32)
        for block in range(views):
            found = jnp.dot(keys[block], q, preferred_element_type=jnp.float32)
            scores[block] = found
            highest = jnp.maximum(highest, jnp.max(found, 0, keepdims=True))
        totals = jnp.zeros((1, length), jnp.float32)
        blended = jnp.zeros((HS, length), jnp.float32)
        for block in range(views):
            weights = jnp.exp(scores[block] - highest)
            totals = totals + jnp.sum(weights, 0, keepdims=True)
            blended = blended + jnp.dot(
                v_ref[block], weights.astype(jnp.bfloat16), preferred_element_type=jnp.float32
            )
        return (blended / totals).astype(jnp.bfloat16)

    def stage(dv):
        attended = attend(lax.rem(view + dv, views))
        for half in range(toks):
            staged[dv, half] = attended[:, half * rows : (half + 1) * rows]

    def copy_to(dv, dt):
        target, half = lax.rem(view + dv, views), lax.rem(tok + dt, toks)
        return pltpu.make_async_remote_copy(
            src_ref=staged.at[dv, half],
            dst_ref=out_ref.at[tok, view],
            send_sem=send_sem.at[dv, dt],
            recv_sem=recv_sem.at[dv, dt],
            device_id={"view": target, "tok": half},
            device_id_type=MESH,
        )

    def one_view(dv, carry):
        stage(dv)
        for dt in range(toks):
            copy_to(dv, dt).start()
        return carry

    lax.fori_loop(1, views, one_view, 0)
    stage(0)
    for dt in range(1, toks):
        copy_to(0, dt).start()
    own = pltpu.make_async_copy(staged.at[0, tok], out_ref.at[tok, view], own_sem)
    own.start()
    for dv, dt in others:
        copy_to(dv, dt).wait_send()
        pltpu.make_async_remote_copy(
            src_ref=staged.at[dv, dt],
            dst_ref=out_ref.at[
                lax.rem(tok - dt + toks, toks), lax.rem(view - dv + views, views)
            ],
            send_sem=send_sem.at[dv, dt],
            recv_sem=recv_sem.at[dv, dt],
            device_id={"view": view, "tok": tok},
            device_id_type=MESH,
        ).wait_recv()
    own.wait()


def attention(queries, keys, values, views, toks):
    length = queries.shape[-1]
    rows = length // toks
    return pl.pallas_call(
        functools.partial(attention_kernel, views, toks),
        out_shape=jax.ShapeDtypeStruct((toks, views, HS, rows), jnp.bfloat16),
        in_specs=[VMEM] * 3,
        out_specs=ANY,
        scratch_shapes=[
            pltpu.VMEM((views, length, HS), jnp.bfloat16),
            pltpu.VMEM((views, length, length), jnp.float32),
            pltpu.VMEM((views, toks, HS, rows), jnp.bfloat16),
            pltpu.SemaphoreType.DMA((views, toks)),
            pltpu.SemaphoreType.DMA((views, toks)),
            pltpu.SemaphoreType.DMA,
        ],
        compiler_params=pltpu.CompilerParams(collective_id=2, has_side_effects=True),
        name="attention",
    )(queries, keys, values)


def by_heads(
    latents,
    query_weight,
    key_weight,
    value_weight,
    output_weight,
    value_units,
    gate_units,
    down_weight,
):
    toks, views = lax.axis_size("tok"), lax.axis_size("view")
    head_width = query_weight.shape[1]
    width = latents.shape[-1]
    stream = latents.reshape(-1, width).astype(jnp.float32)
    rows = stream.shape[0]
    normed = normalize(stream).astype(jnp.bfloat16)
    gathered = over_tokens(normed, toks, False, 0).reshape(toks * rows, width)

    def project(weight):
        return lax.dot_general(
            weight, gathered, (((0,), (1,)), ((), ())), preferred_element_type=jnp.float32
        )

    def heads(projected):
        return projected.astype(jnp.bfloat16).reshape(views, HS, toks * rows)

    queries = heads(project(query_weight) * HS ** (-0.5))
    keys, values = heads(project(key_weight)), heads(project(value_weight))
    queries, keys, values, full_output = spread_heads(
        queries, keys, values, output_weight, views, toks
    )
    attended = attention(queries, keys, values, views, toks).reshape(toks, head_width, rows)
    group_parts = jnp.einsum(
        "gcr,gcd->grd", attended, full_output, preferred_element_type=jnp.float32
    ).astype(jnp.bfloat16)
    middle = stream + jnp.sum(group_parts.astype(jnp.float32), 0)
    normed_two = normalize(middle).astype(jnp.bfloat16)

    def feed(block):
        linear = jnp.dot(block, value_units, preferred_element_type=jnp.float32)
        gating = jnp.dot(block, gate_units, preferred_element_type=jnp.float32)
        hidden = (linear * jax.nn.gelu(gating)).astype(jnp.bfloat16)
        return jnp.dot(hidden, down_weight, preferred_element_type=jnp.float32).astype(jnp.bfloat16)

    pieces = jnp.split(normed_two, 2 if rows % 32 == 0 else 1)
    arrived = [
        [passed_along(piece, "tok", d) for piece in pieces] for d in range(1, toks)
    ]
    total = middle + lax.optimization_barrier(feed(normed_two)).astype(jnp.float32)
    for d, blocks in enumerate(arrived, 1):
        back = [passed_along(feed(block), "tok", -d) for block in blocks]
        total = total + jnp.concatenate(back, 0).astype(jnp.float32)
    return total.astype(jnp.bfloat16).reshape(latents.shape)


def by_ring(
    latents,
    query_weight,
    key_weight,
    value_weight,
    output_weight,
    value_units,
    gate_units,
    down_weight,
):
    stream = latents.astype(jnp.float32)
    normed = normalize(stream).astype(jnp.bfloat16)
    joined = jnp.concatenate([query_weight, key_weight, value_weight], 1)
    projected = jnp.dot(
        lax.all_gather(normed, "tok", axis=0, tiled=True),
        joined,
        preferred_element_type=jnp.float32,
    ).astype(jnp.bfloat16)
    head_width = query_weight.shape[1]
    queries = projected[..., :head_width]
    key_part = projected[..., head_width : 2 * head_width]
    value_part = projected[..., 2 * head_width :]
    length_all, local_views, objects = (queries.shape[0], queries.shape[1], queries.shape[2])
    head_count = head_width // HS
    query_rows = length_all * local_views
    queries_flat = queries.reshape(query_rows, objects, head_count, HS)
    factor = HS ** (-0.5)

    def attend(states, key_block, value_block):
        key_rows = key_block.shape[0]

        def one_view(counter, inner):
            highest, totals, blended = inner
            key_view = lax.dynamic_index_in_dim(key_block, counter, 1, keepdims=False).reshape(
                key_rows, objects, head_count, HS
            )
            value_view = lax.dynamic_index_in_dim(value_block, counter, 1, keepdims=False).reshape(
                key_rows, objects, head_count, HS
            )
            scores = (
                jnp.einsum(
                    "ibhe,jbhe->bhij", queries_flat, key_view, preferred_element_type=jnp.float32
                )
                * factor
            )
            newest = jnp.maximum(highest, jnp.max(scores, -1))
            shrink = jnp.exp(highest - newest)
            weights = jnp.exp(scores - newest[..., None])
            totals = totals * shrink + jnp.sum(weights, -1)
            update = jnp.einsum(
                "bhij,jbhe->bhie",
                weights.astype(jnp.bfloat16),
                value_view,
                preferred_element_type=jnp.float32,
            )
            blended = blended * shrink[..., None] + update
            return (newest, totals, blended)

        return lax.fori_loop(0, key_block.shape[1], one_view, states)

    start_state = (
        jnp.full((objects, head_count, query_rows), -1e30, jnp.float32),
        jnp.zeros((objects, head_count, query_rows), jnp.float32),
        jnp.zeros((objects, head_count, query_rows, HS), jnp.float32),
    )
    stacked = jnp.stack([key_part, value_part])
    states = attend(start_state, key_part, value_part)

    def rotate(counter, bundle):
        inner, buffer_kv = bundle
        buffer_kv = passed_along(buffer_kv, "view", 1)
        return (attend(inner, buffer_kv[0], buffer_kv[1]), buffer_kv)

    states, stacked = lax.fori_loop(0, lax.axis_size("view") - 1, rotate, (states, stacked))
    highest, totals, blended = states
    attended = (blended / totals[..., None]).transpose(2, 0, 1, 3)
    attended = attended.reshape(length_all, local_views, objects, head_width).astype(jnp.bfloat16)
    full_output = lax.all_gather(output_weight, "tok", axis=0, tiled=True)
    own_rows = lax.all_to_all(attended, "tok", split_axis=0, concat_axis=3, tiled=True)
    groups = lax.axis_size("tok")
    grouped = own_rows.reshape(
        own_rows.shape[0], own_rows.shape[1], own_rows.shape[2], groups, head_width
    )
    weight_groups = full_output.reshape(groups, head_width, full_output.shape[1])
    group_parts = jnp.einsum(
        "rvbgc,gcd->rvbgd", grouped, weight_groups, preferred_element_type=jnp.float32
    ).astype(jnp.bfloat16)
    attention_out = jnp.sum(group_parts.astype(jnp.float32), 3)
    middle = stream + attention_out
    normed_two = normalize(middle).astype(jnp.bfloat16)
    gathered = lax.all_gather(normed_two, "tok", axis=0, tiled=True)
    linear = jnp.dot(gathered, value_units, preferred_element_type=jnp.float32)
    gating = jnp.dot(gathered, gate_units, preferred_element_type=jnp.float32)
    hidden = (linear * jax.nn.gelu(gating)).astype(jnp.bfloat16)
    feed_out = lax.psum_scatter(
        jnp.dot(hidden, down_weight, preferred_element_type=jnp.float32).astype(jnp.bfloat16),
        "tok",
        scatter_dimension=0,
        tiled=True,
    ).astype(jnp.float32)
    return (middle + feed_out).astype(jnp.bfloat16)


def on_device(latents, query_weight, *weights):
    head_count = query_weight.shape[1] // HS
    one_each = latents.shape[1] == 1 and latents.shape[2] == 1
    if one_each and head_count == lax.axis_size("view"):
        return by_heads(latents, query_weight, *weights)
    return by_ring(latents, query_weight, *weights)


def solution(mesh):
    return jax.shard_map(
        on_device,
        mesh=mesh,
        in_specs=(
            P("tok", "view", "obj", None),
            P(None, "tok"),
            P(None, "tok"),
            P(None, "tok"),
            P("tok", None),
            P(None, "tok"),
            P(None, "tok"),
            P("tok", None),
        ),
        out_specs=P("tok", "view", "obj", None),
        check_vma=False,
    )
```

profile of v0, /device:TPU:0, one launch (start us, length us, event | category | flops | bytes accessed | tf_op | source)
XLA Modules:
  0.0 156.7 jit_solution(13076310862860998566)
XLA Ops:
  0.0 1.4 convert_reduce_fusion
  1.4 1.4 fusion.16
  2.8 1.2 fusion.17.x_ref
  4.0 18.9 %over_tokens_0.1 = bf16[2,256,1280]{2,1,0:T(8,128)(2,1)} custom-call(bf16[256,1280]{1,0:T(8,128)(2,1)} %fusion.17.x_ref), custom_call_target="tpu_custom_call" | custom-call | tf_op jit(solution)/shard_map/over_tokens_0/pallas_call | solution.py:86
  23.0 0.0 copy-start.5
  23.0 3.2 %fusion.32 = bf16[512,512]{0,1:T(8,128)(2,1)} fusion(bf16[512,1280]{1,0:T(8,128)(2,1)} %bitcast.61, bf16[1280,512]{1,0:T(8,128)(2,1)S(1)} %copy-done), kind=kOutput, calls=%fused_computation.50 | convolution fusion | flops 671612928 | bytes 3145728 | tf_op jit(solution)/shard_map/dot_general | solution.py:250
  26.1 1.7 %convolution_convert_fusion.5 = bf16[512,512]{0,1:T(8,128)(2,1)} fusion(bf16[512,1280]{1,0:T(8,128)(2,1)S(1)} %bitcast.62, bf16[1280,512]{1,0:T(8,128)(2,1)S(1)} %copy-done.5), kind=kOutput, calls=%fused_computation.49 | convolution fusion | flops 671350784 | bytes 3145728 | tf_op jit(solution)/shard_map/dot_general | solution.py:250
  27.8 1.7 %convolution_convert_fusion.4 = bf16[512,512]{0,1:T(8,128)(2,1)} fusion(bf16[512,1280]{1,0:T(8,128)(2,1)S(1)} %bitcast.63, bf16[1280,512]{1,0:T(8,128)(2,1)S(1)} %copy-done.6), kind=kOutput, calls=%fused_computation.48 | convolution fusion | flops 671350784 | bytes 3145728 | tf_op jit(solution)/shard_map/dot_general | solution.py:250
  29.5 37.9 %spread_heads.1 = (bf16[8,64,512]{2,1,0:T(8,128)(2,1)}, bf16[8,64,512]{2,1,0:T(8,128)(2,1)}, bf16[8,64,512]{2,1,0:T(8,128)(2,1)}, bf16[2,512,1280]{2,1,0:T(8,128)(2,1)}) custom-call(bf16[8,64,512]{2,1,0:T(8,128)(2,1)} %bitcast.64, bf16[8,64,512]{2,1,0:T(8,128)(2,1)} %bitcast.65, bf16[8,64,512]{2,1,0:T(8,128)(2,1)} %bitcast.66, bf16[512,1280]{1,0:T(8,128)(2,1)} %w.1), custom_call_target="tpu_custom_call" | custom-call | tf_op jit(solution)/shard_map/spread_heads/pallas_call | solution.py:114
  67.5 34.5 %attention.1 = bf16[2,8,64,256]{3,2,1,0:T(8,128)(2,1)} custom-call(bf16[8,64,512]{2,1,0:T(8,128)(2,1)} %get-tuple-element.9.q_ref, bf16[8,64,512]{2,1,0:T(8,128)(2,1)} %get-tuple-element.10.k_ref, bf16[8,64,512]{2,1,0:T(8,128)(2,1)} %get-tuple-element.11.v_ref), custom_call_target="tpu_custom_call" | custom-call | tf_op jit(solution)/shard_map/attention/pallas_call | solution.py:213
  102.0 0.0 slice-start
  102.0 3.0 %fusion.13 = f32[256,1280]{1,0:T(8,128)S(1)} fusion(bf16[2,512,256]{2,1,0:T(8,128)(2,1)} %bitcast.60, bf16[2,512,1280]{2,1,0:T(8,128)(2,1)} %get-tuple-element.12), kind=kOutput, calls=%fused_computation.25 | convolution fusion | flops 672727040 | bytes 4456448 | tf_op jit(solution)/shard_map/gcr,gcd->grd/dot_general | solution.py:263
  105.0 0.0 slice-start.1
  105.0 0.2 fusion.34
  105.3 0.3 multiply_reduce_fusion
  105.6 0.2 multiply_convert_fusion
  105.8 0.0 copy-start.2
  105.8 0.8 fusion.47
  106.7 1.5 collective-permute-start.2
  108.2 0.6 collective-permute-start
  108.7 3.4 %fusion.48 = f32[256,2560]{1,0:T(8,128)} fusion(bf16[256,1280]{1,0:T(8,128)(2,1)S(1)} %multiply_convert_fusion, bf16[1280,2560]{1,0:T(8,128)(2,1)S(1)} %bitcast.59), kind=kOutput, calls=%fused_computation.70 | convolution fusion | flops 1677721600 | bytes 9830400 | tf_op jit(solution)/shard_map/dot_general | solution.py:271
  112.1 5.2 %collective-permute-done.2 = bf16[128,1280]{1,0:T(8,128)(2,1)S(1)} collective-permute-done((bf16[128,1280]{1,0:T(8,128)(2,1)S(1)}, bf16[128,1280]{1,0:T(8,128)(2,1)S(1)}, u32[]{:S(2)}, u32[]{:S(2)}) %collective-permute-start.2) | collective-permute-done | bytes 327712 | tf_op jit(solution)/shard_map/ppermute | solution.py:22
  117.3 0.7 copy-done.4
  118.0 2.1 %fusion.50 = f32[128,2560]{1,0:T(8,128)} fusion(bf16[128,1280]{1,0:T(8,128)(2,1)S(1)} %collective-permute-done.2, bf16[1280,2560]{1,0:T(8,128)(2,1)S(1)} %bitcast.59), kind=kOutput, calls=%fused_computation.72 | convolution fusion | flops 838860800 | bytes 8192000 | tf_op jit(solution)/shard_map/dot_general | solution.py:271
  120.1 8.3 %convolution_convert_fusion.2 = bf16[128,1280]{1,0:T(8,128)(2,1)} fusion(bf16[2560,1280]{1,0:T(8,128)(2,1)} %param.15, bf16[128,1280]{1,0:T(8,128)(2,1)} %copy-done.4, bf16[1280,2560]{1,0:T(8,128)(2,1)} %param.13, f32[128,2560]{1,0:T(8,128)} %fusion.50), kind=kOutput, calls=%fused_computation.17 | convolution fusion | flops 1681162240 | bytes 15073280 | tf_op jit(solution)/shard_map/dot_general | solution.py:273
  128.4 1.5 collective-permute-start.3
  129.9 5.1 %fusion.49 = f32[128,2560]{1,0:T(8,128)} fusion(bf16[128,1280]{1,0:T(8,128)(2,1)} %collective-permute-done, bf16[1280,2560]{1,0:T(8,128)(2,1)} %param.14), kind=kOutput, calls=%fused_computation.71 | convolution fusion | flops 838860800 | bytes 8192000 | tf_op jit(solution)/shard_map/dot_general | solution.py:271
  135.0 8.3 %convolution_convert_fusion.3 = bf16[128,1280]{1,0:T(8,128)(2,1)} fusion(bf16[2560,1280]{1,0:T(8,128)(2,1)} %param.15, bf16[128,1280]{1,0:T(8,128)(2,1)} %collective-permute-done, bf16[1280,2560]{1,0:T(8,128)(2,1)} %param.13, f32[128,2560]{1,0:T(8,128)} %fusion.49), kind=kOutput, calls=%fused_computation.18 | convolution fusion | flops 1681162240 | bytes 15073280 | tf_op jit(solution)/shard_map/dot_general | solution.py:273
  143.3 0.6 collective-permute-start.1
  143.9 10.5 %convolution_convert_fusion.1 = bf16[256,1280]{1,0:T(8,128)(2,1)} fusion(bf16[2560,1280]{1,0:T(8,128)(2,1)} %param.15, bf16[256,1280]{1,0:T(8,128)(2,1)} %copy-done.2, bf16[1280,2560]{1,0:T(8,128)(2,1)} %param.13, f32[256,2560]{1,0:T(8,128)} %fusion.48), kind=kOutput, calls=%fused_computation.16 | convolution fusion | flops 3362324480 | bytes 17039360 | tf_op jit(solution)/shard_map/dot_general | solution.py:273
  154.3 0.0 collective-permute-done.3
  154.3 2.4 %fusion.33 = bf16[256,1,1,1280]{3,0,2,1:T(8,128)(2,1)} fusion(bf16[256,1280]{1,0:T(8,128)(2,1)} %convolution_convert_fusion.1, bf16[128,1280]{1,0:T(8,128)(2,1)} %collective-permute-done.3, bf16[128,1280]{1,0:T(8,128)(2,1)} %collective-permute-done.1, f32[256,1280]{1,0:T(8,128)S(1)} %fusion.13, bf16[256,1,1,1280]{3,0,2,1:T(8,128)(2,1)S(1)} %copy-done.1), kind=kLoop, calls=%fused_computation.51 | loop fusion | flops 3276800 | bytes 3932160 | tf_op jit(solution)/shard_map/reshape | solution.py:283
  (20 shorter events, 0.1 us)
Async XLA Ops:
  0.0 22.9 %copy-start = (bf16[1280,512]{1,0:T(8,128)(2,1)S(1)}, bf16[1280,512]{1,0:T(8,128)(2,1)}, u32[]{:S(2)}) copy-start(bf16[1280,512]{1,0:T(8,128)(2,1)} %param.9) | copy-start | bytes 3932164
  0.0 2.8 %copy-start.1 = (bf16[256,1,1,1280]{3,0,2,1:T(8,128)(2,1)S(1)}, bf16[256,1,1,1280]{3,0,2,1:T(8,128)(2,1)}, u32[]{:S(2)}) copy-start(bf16[256,1,1,1280]{3,0,2,1:T(8,128)(2,1)} %param.8) | copy-start | bytes 1966084
  23.0 3.2 %copy-start.3 = (bf16[2,256,1280]{2,1,0:T(8,128)(2,1)S(1)}, bf16[2,256,1280]{2,1,0:T(8,128)(2,1)}, u32[]{:S(2)}) copy-start(bf16[2,256,1280]{2,1,0:T(8,128)(2,1)} %over_tokens_0.1) | copy-start | bytes 3932164
  23.0 3.2 %copy-start.5 = (bf16[1280,512]{1,0:T(8,128)(2,1)S(1)}, bf16[1280,512]{1,0:T(8,128)(2,1)}, u32[]{:S(2)}) copy-start(bf16[1280,512]{1,0:T(8,128)(2,1)} %param.10) | copy-start | bytes 3932164
  26.1 1.7 %copy-start.6 = (bf16[1280,512]{1,0:T(8,128)(2,1)S(1)}, bf16[1280,512]{1,0:T(8,128)(2,1)}, u32[]{:S(2)}) copy-start(bf16[1280,512]{1,0:T(8,128)(2,1)} %param.11) | copy-start | bytes 3932164
  102.0 6.7 %slice-start = ((s8[6553600]{0:T(1024)(128)(4,1)}), s8[4194304]{0:T(1024)(128)(4,1)S(1)}, s32[]{:S(2)}) async-start(s8[6553600]{0:T(1024)(128)(4,1)} %bitcast.58), calls=%async_computation | async-start | bytes 8388608
  105.0 3.7 %slice-start.1 = ((s8[6553600]{0:T(1024)(128)(4,1)}), s8[2359296]{0:T(1024)(128)(4,1)S(1)}, s32[]{:S(2)}) async-start(s8[6553600]{0:T(1024)(128)(4,1)} %bitcast.58), calls=%async_computation.1 | async-start | bytes 4718592
  105.8 6.3 %copy-start.2 = (bf16[256,1280]{1,0:T(8,128)(2,1)}, bf16[256,1280]{1,0:T(8,128)(2,1)S(1)}, u32[]{:S(2)}) copy-start(bf16[256,1280]{1,0:T(8,128)(2,1)S(1)} %multiply_convert_fusion) | copy-start | bytes 1966084
  106.7 10.6 %collective-permute-start.2 = (bf16[128,1280]{1,0:T(8,128)(2,1)S(1)}, bf16[128,1280]{1,0:T(8,128)(2,1)S(1)}, u32[]{:S(2)}, u32[]{:S(2)}) collective-permute-start(bf16[128,1280]{1,0:T(8,128)(2,1)S(1)} %get-tuple-element.14), channel_id=1, source_target_pairs={{2,0},{0,2},{3,1},{1,3},{6,4},{4,6},{7,5},{5,7},{10,8},{8,10},{11,... | collective-permute-start | bytes 983048 | tf_op jit(solution)/shard_map/ppermute | solution.py:22
  108.2 21.7 %collective-permute-start = (bf16[128,1280]{1,0:T(8,128)(2,1)}, bf16[128,1280]{1,0:T(8,128)(2,1)}, u32[]{:S(2)}, u32[]{:S(2)}) collective-permute-start(bf16[128,1280]{1,0:T(8,128)(2,1)} %get-tuple-element.13), channel_id=1, source_target_pairs={{2,0},{0,2},{3,1},{1,3},{6,4},{4,6},{7,5},{5,7},{10,8},{8,10},{11,... | collective-permute-start | bytes 983048 | tf_op jit(solution)/shard_map/ppermute | solution.py:22
  117.3 0.7 copy-start.4
  128.4 25.9 %collective-permute-start.3 = (bf16[128,1280]{1,0:T(8,128)(2,1)}, bf16[128,1280]{1,0:T(8,128)(2,1)}, u32[]{:S(2)}, u32[]{:S(2)}) collective-permute-start(bf16[128,1280]{1,0:T(8,128)(2,1)} %convolution_convert_fusion.2), channel_id=1, source_target_pairs={{2,0},{0,2},{3,1},{1,3},{6,4},{4,6},{7,5},{5,7},{10,8},{8,10},{11,... | collective-permute-start | bytes 983048 | tf_op jit(solution)/shard_map/ppermute | solution.py:22
  143.3 11.0 %collective-permute-start.1 = (bf16[128,1280]{1,0:T(8,128)(2,1)}, bf16[128,1280]{1,0:T(8,128)(2,1)}, u32[]{:S(2)}, u32[]{:S(2)}) collective-permute-start(bf16[128,1280]{1,0:T(8,128)(2,1)} %convolution_convert_fusion.3), channel_id=1, source_target_pairs={{2,0},{0,2},{3,1},{1,3},{6,4},{4,6},{7,5},{5,7},{10,8},{8,10},{11,... | collective-permute-start | bytes 983048 | tf_op jit(solution)/shard_map/ppermute | solution.py:22
where the time goes:
time: 157 us
  Pallas kernels  91.4 us (58%)
  matrix products  47.3 us (30%)
  other arithmetic  7.14 us (5%)
  waiting for transfers between devices  5.19 us (3%)
  starting transfers between devices  4.05 us (3%)
  local copies, waits for them, and re-layouts  1.6 us (1%)
    pallas_call x1, Pallas kernels, spread_heads(): pl.pallas_call(functools.partial(heads_kernel, views, toks), out_shape=(l...  37.9 us
    pallas_call x1, Pallas kernels, attention(): pl.pallas_call(functools.partial(attention_kernel, views, toks), out_shap...  34.5 us
    dot_general x3, matrix products, feed(): jnp.dot(hidden, down_weight, preferred_element_type=jnp.float32)  27.1 us
    pallas_call x1, Pallas kernels, over_tokens(): pl.pallas_call(functools.partial(token_kernel, count, scattered), out_sha...  18.9 us
    dot_general x3, matrix products, feed(): gating = jnp.dot(block, gate_units, preferred_element_type=jnp.float32)  10.5 us
    dot_general x3, matrix products, project(): lax.dot_general(weight, gathered, (((0,), (1,)), ((), ())), preferred_ele...  6.55 us
    ppermute x4, waiting for transfers between devices, passed_along(): return lax.ppermute(block, axis, route)  5.19 us
    ppermute x4, starting transfers between devices, passed_along(): return lax.ppermute(block, axis, route)  4.05 us
  transfers between devices with their start and end apart: 4, of which 1 were waited for; matrix products, arithmetic and copies ran while one was open for 24% of the time, Pallas kernels for 0%

commit v1 on v0

v1 whole, which is shorter than its diff:
```python
import functools
import math

import jax
import jax.numpy as jnp
from jax import lax
from jax.experimental import pallas as pl
from jax.experimental.pallas import tpu as pltpu
from jax.sharding import PartitionSpec as P

HS = 64
ONES = 16
CHUNK = 256
MESH = pl.DeviceIdType.MESH
ANY = pl.BlockSpec(memory_space=pl.ANY)
F32, BF16 = jnp.float32, jnp.bfloat16


epsilon = 1e-05


def passed_along(block, axis, distance):
    devices = range(lax.axis_size(axis))
    route = [((i - distance) % len(devices), i) for i in devices]
    return lax.ppermute(block, axis, route)


def normalize(stream):
    average = jnp.mean(stream, -1, keepdims=True)
    centered = stream - average
    spread = jnp.mean(centered * centered, -1, keepdims=True)
    return centered * lax.rsqrt(spread + epsilon)


def gelu(v):
    return 0.5 * v * (1.0 + jnp.tanh(math.sqrt(2.0 / math.pi) * (v + 0.044715 * (v * v * v))))


def block_kernel(
    views,
    latents,
    query_weight,
    key_weight,
    value_weight,
    output_weight,
    value_units,
    gate_units,
    down_weight,
    out_ref,
    rows_in,
    wq,
    wk,
    wv,
    wo,
    vu,
    gu,
    dw,
    normed,
    send_q,
    send_kv,
    q_all,
    kv_all,
    keys,
    vals,
    scores_a,
    scores_b,
    staged,
    att,
    middle,
    hidden,
    part_own,
    part_out,
    part_in,
    load_sem,
    lat_sem,
    kv_sem,
    q_sem,
    wo_sem,
    att_sem,
    relay_sem,
    part_sem,
):
    view, tok, obj = lax.axis_index("view"), lax.axis_index("tok"), lax.axis_index("obj")
    other, twin = 1 - tok, 1 - obj
    rows = rows_in.shape[1]
    width = rows_in.shape[2]
    half_of = (tok, other)

    def load(number, source, target):
        return pltpu.make_async_copy(source, target, load_sem.at[number])

    loads = [
        load(0, latents, rows_in.at[0]),
        load(1, key_weight, wk),
        load(2, value_weight, wv),
        load(3, query_weight, wq),
        load(4, output_weight, wo.at[tok]),
        load(5, value_units, vu),
        load(6, gate_units, gu),
        load(7, down_weight, dw),
    ]
    for item in loads[:4]:
        item.start()

    barrier = pltpu.get_barrier_semaphore()
    for d in range(1, views):
        pl.semaphore_signal(
            barrier, inc=1, device_id={"view": lax.rem(view + d, views)}, device_id_type=MESH
        )
    pl.semaphore_signal(barrier, inc=1, device_id={"tok": other}, device_id_type=MESH)
    pl.semaphore_signal(barrier, inc=1, device_id={"obj": twin}, device_id_type=MESH)

    def remote(source, target, sems, index, device):
        return pltpu.make_async_remote_copy(
            src_ref=source,
            dst_ref=target,
            send_sem=sems.at[(0,) + index],
            recv_sem=sems.at[(1,) + index],
            device_id=device,
            device_id_type=MESH,
        )

    lat_copy = remote(rows_in.at[0], rows_in.at[1], lat_sem, (), {"tok": other})

    loads[0].wait()
    normed[...] = normalize(rows_in[0].astype(F32)).astype(BF16)
    pl.semaphore_wait(barrier, views + 1)
    lat_copy.start()

    far_first = sorted(range(1, views), key=lambda d: abs(d - views // 2))

    def kv_copy(slot, d):
        peer = lax.rem(view + d, views)
        return remote(
            send_kv.at[slot, peer], kv_all.at[slot, view], kv_sem, (slot, d), {"view": peer}
        )

    def q_copy(slot, d):
        peer = lax.rem(view + d, views)
        return remote(send_q.at[slot, peer], q_all.at[slot, view], q_sem, (slot, d), {"view": peer})

    def kv_arrival(slot, d):
        source = lax.rem(view - d + views, views)
        return remote(
            send_kv.at[slot, source], kv_all.at[slot, source], kv_sem, (slot, d), {"view": source}
        )

    def q_arrival(slot, d):
        source = lax.rem(view - d + views, views)
        return remote(
            send_q.at[slot, source], q_all.at[slot, source], q_sem, (slot, d), {"view": source}
        )

    def project(weight):
        return jnp.dot(normed[...], weight[...], preferred_element_type=F32)

    def turned(projected):
        return projected.astype(BF16).T.reshape(views, HS, rows)

    def spread_kv(slot):
        send_kv[slot, :, 0] = turned(project(wk))
        send_kv[slot, :, 1] = turned(project(wv))
        for d in far_first:
            kv_copy(slot, d).start()
        kv_all[slot, view] = send_kv[slot, view]

    def spread_q(slot):
        send_q[slot] = turned(project(wq) * (HS**-0.5 * math.log2(math.e)))
        for d in far_first:
            q_copy(slot, d).start()
        q_all[slot, view] = send_q[slot, view]

    loads[1].wait()
    loads[2].wait()
    spread_kv(0)
    loads[3].wait()
    for item in loads[4:]:
        item.start()
    spread_q(0)

    lat_copy.wait_recv()
    loads[4].wait()
    share = wo.shape[1] // 2
    mine, theirs = pl.ds(obj * share, share), pl.ds(twin * share, share)
    wo_across = remote(wo.at[tok, mine], wo.at[tok, mine], wo_sem, (0,), {"tok": other})
    wo_across.start()
    normed[...] = normalize(rows_in[1].astype(F32)).astype(BF16)
    spread_kv(1)
    spread_q(1)

    vals[:, :, HS:, :] = jnp.ones((2, views, ONES, rows), BF16)

    def prepare(slot):
        def one(d, carry):
            source = lax.rem(view - d + views, views)

            @pl.when(d > 0)
            def _():
                kv_arrival(slot, d).wait_recv()

            keys[slot, source] = kv_all[slot, source, 0].T
            vals[slot, source, :HS, :] = kv_all[slot, source, 1]
            return carry

        lax.fori_loop(0, views, one, 0)

    prepare(0)
    prepare(1)

    steps = 2 * views
    blocks = [(slot, number) for slot in range(2) for number in range(views)]

    def place(n):
        slot, turn = n // views, lax.rem(n, views) + 1
        return slot, turn, lax.rem(view + turn, views)

    def fetch_q(n):
        slot, turn, target = place(n)

        @pl.when(turn != views)
        def _():
            q_arrival(slot, views - turn).wait_recv()

    def att_copy(n):
        slot, turn, target = place(n)
        half = jnp.where(slot == 0, tok, other)
        return remote(
            staged.at[slot, target],
            att.at[half, tok, view],
            att_sem,
            (slot, turn),
            {"view": target},
        )

    def att_arrival(n):
        slot, turn, _ = place(n)
        half = jnp.where(slot == 0, tok, other)
        source = lax.rem(view - turn + views, views)
        return remote(
            staged.at[slot, source],
            att.at[half, tok, source],
            att_sem,
            (slot, turn),
            {"view": source},
        )

    def relay_copy(n):
        slot, turn, _ = place(n)
        half = jnp.where(slot == 0, tok, other)
        source = lax.rem(view - turn + views, views)
        return remote(
            att.at[half, tok, source],
            att.at[half, tok, source],
            relay_sem,
            (slot, turn),
            {"tok": other},
        )

    def relay_arrival(n):
        slot, turn, _ = place(n)
        half = jnp.where(slot == 0, other, tok)
        source = lax.rem(view - turn + views, views)
        return remote(
            att.at[half, other, source],
            att.at[half, other, source],
            relay_sem,
            (slot, turn),
            {"tok": other},
        )

    def score(n, buffer, number):
        slot, turn, target = place(n)
        found = jnp.dot(
            keys[blocks[number]], q_all[slot, target], preferred_element_type=F32
        )
        buffer[number] = found
        return jnp.max(found, 0, keepdims=True)

    def blend(buffer, highest, number):
        weights = jnp.exp2(buffer[number] - highest).astype(BF16)
        return jnp.dot(vals[blocks[number]], weights, preferred_element_type=F32)

    def unit(n, current, highest, following):
        blended = jnp.zeros((HS + ONES, rows), F32)
        upcoming = jnp.full((1, rows), -1e30, F32)
        for number in range(steps):
            if following is not None:
                upcoming = jnp.maximum(upcoming, score(n + 1, following, number))
            blended = blended + blend(current, highest, number)
        result = (blended[:HS] / blended[HS : HS + 1]).astype(BF16)
        slot, turn, target = place(n)
        staged[slot, target] = result
        return upcoming

    def post(n):
        slot, turn, target = place(n)
        half = jnp.where(slot == 0, tok, other)

        @pl.when(turn != views)
        def _():
            att_copy(n).start()

        @pl.when(turn == views)
        def _():
            att[half, tok, view] = staged[slot, view]

    def relay(n):
        slot, turn, target = place(n)

        @pl.when(turn != views)
        def _():
            att_arrival(n).wait_recv()

        relay_copy(n).start()

    def first_scores():
        fetch_q(0)
        highest = jnp.full((1, rows), -1e30, F32)
        for number in range(steps):
            highest = jnp.maximum(highest, score(0, scores_a, number))
        return highest

    LAG = 2

    def two_steps(i, highest):
        n = 2 * i
        fetch_q(n + 1)
        highest = unit(n, scores_a, highest, scores_b)
        post(n)

        @pl.when(n >= LAG)
        def _():
            relay(n - LAG)

        fetch_q(n + 2)
        highest = unit(n + 1, scores_b, highest, scores_a)
        post(n + 1)

        @pl.when(n + 1 >= LAG)
        def _():
            relay(n + 1 - LAG)

        return highest

    highest = first_scores()
    highest = lax.fori_loop(0, views - 1, two_steps, highest)
    last = steps - 2
    fetch_q(last + 1)
    highest = unit(last, scores_a, highest, scores_b)
    post(last)
    relay(last - LAG)
    wo_arrival = remote(wo.at[other, mine], wo.at[other, mine], wo_sem, (0,), {"tok": other})
    wo_arrival.wait_recv()
    wo_swap = remote(wo.at[other, mine], wo.at[other, mine], wo_sem, (1,), {"obj": twin})
    wo_swap.start()
    unit(last + 1, scores_b, highest, None)
    post(last + 1)
    relay(last + 1 - LAG)
    relay(last)
    relay(last + 1)

    remote(wo.at[other, theirs], wo.at[other, theirs], wo_sem, (1,), {"obj": twin}).wait_recv()

    columns = width // CHUNK

    def join(slot):
        half = half_of[slot]
        gathered = att[half].reshape(2 * views * HS, rows).T

        def one(c, carry):
            at = pl.ds(pl.multiple_of(c * CHUNK, CHUNK), CHUNK)
            whole = wo[:, :, at].reshape(2 * views * HS, CHUNK)
            middle[slot, :, at] = rows_in[slot, :, at].astype(F32) + jnp.dot(
                gathered, whole, preferred_element_type=F32
            )
            return carry

        lax.fori_loop(0, columns, one, 0)
        normed[...] = normalize(middle[slot]).astype(BF16)

    def units():
        wide = 2 * CHUNK

        def one(c, carry):
            at = pl.ds(pl.multiple_of(c * wide, wide), wide)
            block = normed[...]
            linear = jnp.dot(block, vu[:, at], preferred_element_type=F32)
            gating = jnp.dot(block, gu[:, at], preferred_element_type=F32)
            hidden[:, at] = (linear * gelu(gating)).astype(BF16)
            return carry

        lax.fori_loop(0, hidden.shape[1] // wide, one, 0)

    def down(c):
        at = pl.ds(pl.multiple_of(c * CHUNK, CHUNK), CHUNK)
        return jnp.dot(hidden[...], dw[:, at], preferred_element_type=F32)

    def part_copy(c):
        return remote(part_out.at[c], part_in.at[c], part_sem, (c,), {"tok": other})

    def wait_relays(first):
        def one(n, carry):
            relay_arrival(first + n).wait_recv()
            return carry

        lax.fori_loop(0, views, one, 0)

    wait_relays(0)
    join(1)
    for item in loads[5:]:
        item.wait()
    units()

    def send_part(c, carry):
        part_out[c] = down(c).astype(BF16)
        part_copy(c).start()
        return carry

    lax.fori_loop(0, columns, send_part, 0)
    wait_relays(views)
    join(0)
    units()

    def keep_part(c, carry):
        part_own[c] = down(c)
        return carry

    lax.fori_loop(0, columns, keep_part, 0)

    for c in range(columns):
        part_copy(c).wait_recv()
        at = slice(c * CHUNK, (c + 1) * CHUNK)
        total = middle[0, :, at] + part_own[c] + part_in[c].astype(F32)
        out_ref[:, at] = total.astype(BF16)

    lat_copy.wait_send()
    wo_across.wait_send()
    wo_swap.wait_send()

    def drain(d, carry):
        for slot in range(2):
            kv_copy(slot, d).wait_send()
            q_copy(slot, d).wait_send()
            att_copy(slot * views + d - 1).wait_send()
        return carry

    lax.fori_loop(1, views, drain, 0)

    def drain_relays(n, carry):
        relay_copy(n).wait_send()
        return carry

    lax.fori_loop(0, steps, drain_relays, 0)

    def drain_parts(c, carry):
        part_copy(c).wait_send()
        return carry

    lax.fori_loop(0, columns, drain_parts, 0)


def by_heads(latents, *weights):
    views = lax.axis_size("view")
    width = latents.shape[-1]
    stream = latents.reshape(-1, width)
    rows = stream.shape[0]
    head_width, units = weights[0].shape[1], weights[4].shape[1]
    columns = width // CHUNK
    half = (2, views)
    dma = pltpu.SemaphoreType.DMA
    scratch = [
        pltpu.VMEM((2, rows, width), BF16),
        pltpu.VMEM((width, head_width), BF16),
        pltpu.VMEM((width, head_width), BF16),
        pltpu.VMEM((width, head_width), BF16),
        pltpu.VMEM((2, head_width, width), BF16),
        pltpu.VMEM((width, units), BF16),
        pltpu.VMEM((width, units), BF16),
        pltpu.VMEM((units, width), BF16),
        pltpu.VMEM((rows, width), BF16),
        pltpu.VMEM(half + (HS, rows), BF16),
        pltpu.VMEM(half + (2, HS, rows), BF16),
        pltpu.VMEM(half + (HS, rows), BF16),
        pltpu.VMEM(half + (2, HS, rows), BF16),
        pltpu.VMEM(half + (rows, HS), BF16),
        pltpu.VMEM(half + (HS + ONES, rows), BF16),
        pltpu.VMEM((2 * views, rows, rows), F32),
        pltpu.VMEM((2 * views, rows, rows), F32),
        pltpu.VMEM(half + (HS, rows), BF16),
        pltpu.VMEM((2, 2, views, HS, rows), BF16),
        pltpu.VMEM((2, rows, width), F32),
        pltpu.VMEM((rows, units), BF16),
        pltpu.VMEM((columns, rows, CHUNK), F32),
        pltpu.VMEM((columns, rows, CHUNK), BF16),
        pltpu.VMEM((columns, rows, CHUNK), BF16),
        dma((8,)),
        dma((2,)),
        dma((2, 2, views)),
        dma((2, 2, views)),
        dma((2, 2)),
        dma((2, 2, views + 1)),
        dma((2, 2, views + 1)),
        dma((2, columns)),
    ]
    result = pl.pallas_call(
        functools.partial(block_kernel, views),
        out_shape=jax.ShapeDtypeStruct((rows, width), BF16),
        in_specs=[ANY] * 8,
        out_specs=pl.BlockSpec(memory_space=pltpu.VMEM),
        scratch_shapes=scratch,
        compiler_params=pltpu.CompilerParams(
            collective_id=0, has_side_effects=True, vmem_limit_bytes=62 * 1024 * 1024
        ),
        name="block",
    )(stream, *weights)
    return result.reshape(latents.shape)


def by_ring(
    latents,
    query_weight,
    key_weight,
    value_weight,
    output_weight,
    value_units,
    gate_units,
    down_weight,
):
    stream = latents.astype(jnp.float32)
    normed = normalize(stream).astype(jnp.bfloat16)
    joined = jnp.concatenate([query_weight, key_weight, value_weight], 1)
    projected = jnp.dot(
        lax.all_gather(normed, "tok", axis=0, tiled=True),
        joined,
        preferred_element_type=jnp.float32,
    ).astype(jnp.bfloat16)
    head_width = query_weight.shape[1]
    queries = projected[..., :head_width]
    key_part = projected[..., head_width : 2 * head_width]
    value_part = projected[..., 2 * head_width :]
    length_all, local_views, objects = (queries.shape[0], queries.shape[1], queries.shape[2])
    head_count = head_width // HS
    query_rows = length_all * local_views
    queries_flat = queries.reshape(query_rows, objects, head_count, HS)
    factor = HS ** (-0.5)

    def attend(states, key_block, value_block):
        key_rows = key_block.shape[0]

        def one_view(counter, inner):
            highest, totals, blended = inner
            key_view = lax.dynamic_index_in_dim(key_block, counter, 1, keepdims=False).reshape(
                key_rows, objects, head_count, HS
            )
            value_view = lax.dynamic_index_in_dim(value_block, counter, 1, keepdims=False).reshape(
                key_rows, objects, head_count, HS
            )
            scores = (
                jnp.einsum(
                    "ibhe,jbhe->bhij", queries_flat, key_view, preferred_element_type=jnp.float32
                )
                * factor
            )
            newest = jnp.maximum(highest, jnp.max(scores, -1))
            shrink = jnp.exp(highest - newest)
            weights = jnp.exp(scores - newest[..., None])
            totals = totals * shrink + jnp.sum(weights, -1)
            update = jnp.einsum(
                "bhij,jbhe->bhie",
                weights.astype(jnp.bfloat16),
                value_view,
                preferred_element_type=jnp.float32,
            )
            blended = blended * shrink[..., None] + update
            return (newest, totals, blended)

        return lax.fori_loop(0, key_block.shape[1], one_view, states)

    start_state = (
        jnp.full((objects, head_count, query_rows), -1e30, jnp.float32),
        jnp.zeros((objects, head_count, query_rows), jnp.float32),
        jnp.zeros((objects, head_count, query_rows, HS), jnp.float32),
    )
    stacked = jnp.stack([key_part, value_part])
    states = attend(start_state, key_part, value_part)

    def rotate(counter, bundle):
        inner, buffer_kv = bundle
        buffer_kv = passed_along(buffer_kv, "view", 1)
        return (attend(inner, buffer_kv[0], buffer_kv[1]), buffer_kv)

    states, stacked = lax.fori_loop(0, lax.axis_size("view") - 1, rotate, (states, stacked))
    highest, totals, blended = states
    attended = (blended / totals[..., None]).transpose(2, 0, 1, 3)
    attended = attended.reshape(length_all, local_views, objects, head_width).astype(jnp.bfloat16)
    full_output = lax.all_gather(output_weight, "tok", axis=0, tiled=True)
    own_rows = lax.all_to_all(attended, "tok", split_axis=0, concat_axis=3, tiled=True)
    groups = lax.axis_size("tok")
    grouped = own_rows.reshape(
        own_rows.shape[0], own_rows.shape[1], own_rows.shape[2], groups, head_width
    )
    weight_groups = full_output.reshape(groups, head_width, full_output.shape[1])
    group_parts = jnp.einsum(
        "rvbgc,gcd->rvbgd", grouped, weight_groups, preferred_element_type=jnp.float32
    ).astype(jnp.bfloat16)
    attention_out = jnp.sum(group_parts.astype(jnp.float32), 3)
    middle = stream + attention_out
    normed_two = normalize(middle).astype(jnp.bfloat16)
    gathered = lax.all_gather(normed_two, "tok", axis=0, tiled=True)
    linear = jnp.dot(gathered, value_units, preferred_element_type=jnp.float32)
    gating = jnp.dot(gathered, gate_units, preferred_element_type=jnp.float32)
    hidden = (linear * jax.nn.gelu(gating)).astype(jnp.bfloat16)
    feed_out = lax.psum_scatter(
        jnp.dot(hidden, down_weight, preferred_element_type=jnp.float32).astype(jnp.bfloat16),
        "tok",
        scatter_dimension=0,
        tiled=True,
    ).astype(jnp.float32)
    return (middle + feed_out).astype(jnp.bfloat16)


def on_device(latents, query_weight, *weights):
    rows, width = latents.shape[0], latents.shape[-1]
    head_width, unit_width = query_weight.shape[1], weights[3].shape[1]
    fits = (
        latents.shape[1] == 1
        and latents.shape[2] == 1
        and head_width == lax.axis_size("view") * HS
        and lax.axis_size("tok") == 2
        and lax.axis_size("obj") == 2
        and rows == CHUNK
        and width % CHUNK == 0
        and unit_width % (2 * CHUNK) == 0
    )
    if fits:
        return by_heads(latents, query_weight, *weights)
    return by_ring(latents, query_weight, *weights)


def solution(mesh):
    return jax.shard_map(
        on_device,
        mesh=mesh,
        in_specs=(
            P("tok", "view", "obj", None),
            P(None, "tok"),
            P(None, "tok"),
            P(None, "tok"),
            P("tok", None),
            P(None, "tok"),
            P(None, "tok"),
            P("tok", None),
        ),
        out_specs=P("tok", "view", "obj", None),
        check_vma=False,
    )
```

time: 157 us -> 92.7 us (0.59)
  matrix products: 47.3 us -> 0 us
  other arithmetic: 7.14 us -> 0 us
  waiting for transfers between devices: 5.19 us -> 0 us
  starting transfers between devices: 4.05 us -> 0 us
    dot_general x10 -> x0, matrix products: 47.3 us -> none  [the longest x3 27.1 us: feed(): jnp.dot(hidden, down_weight, preferred_element_type=jnp.float32)]
    ppermute x4 -> x0, waiting for transfers between devices: 5.19 us -> none  [passed_along(): return lax.ppermute(block, axis, route)]
    ppermute x4 -> x0, starting transfers between devices: 4.05 us -> none  [passed_along(): return lax.ppermute(block, axis, route)]
    reduce_sum x4 -> x0, other arithmetic: 3.33 us -> none  [the longest x2 1.72 us: normalize(): spread = jnp.mean(centered * centered, -1, keepdims=True)]
    reshape x1 -> x0, other arithmetic: 2.38 us -> none  [by_heads(): return total.astype(jnp.bfloat16).reshape(latents.shape)]
    pallas_call x3 -> x1, Pallas kernels: 91.4 us -> 90.6 us  [by_heads(): pl.pallas_call(functools.partial(block_kernel, views), out_shape=jax.Shap...]
  transfers between devices with their start and end apart: 4 -> 0, of which waited for: 1 -> 0; matrix products, arithmetic and copies ran while one was open for 24% -> 0% of each run, Pallas kernels for 0% -> 0%
where the time goes in v1:
time: 92.7 us; the launch traced here: 92.6 us
  Pallas kernels  90.6 us (98%)
  local copies, waits for them, and re-layouts  1.97 us (2%)
    pallas_call x1, Pallas kernels, by_heads(): pl.pallas_call(functools.partial(block_kernel, views), out_shape=jax.Shap...  90.6 us
    unnamed x1, local copies, waits for them, and re-layouts  1.97 us

profile of v1, /device:TPU:0, one launch (start us, length us, event | category | flops | bytes accessed | tf_op | source)
XLA Modules:
  0.0 92.6 jit_solution(8195378325017404644)
XLA Ops:
  0.0 90.6 %block.1 = bf16[256,1280]{1,0:T(8,128)(2,1)} custom-call(bf16[256,1280]{1,0:T(8,128)(2,1)} %bitcast.3, bf16[1280,512]{1,0:T(8,128)(2,1)} %query_weight.1, bf16[1280,512]{1,0:T(8,128)(2,1)} %key_weight.1, bf16[1280,512]{1,0:T(8,128)(2,1)} %value_weight.1, bf16[512,1280]{1,0:T(8,128)(2,1)} %output_weight.1, bf16[1280,2560]{1,0:T(8,128)(2,1)} %value_units.1, ...), custom_call_target="tpu_custom_call" | custom-call | tf_op jit(solution)/shard_map/block/pallas_call | solution.py:505
  90.6 2.0 %copy.10 = bf16[256,1,1,1280]{3,0,2,1:T(8,128)(2,1)} copy(bf16[256,1,1,1280]{3,0,2,1:T(8,128)(2,1)} %bitcast.2) | data formatting | bytes 1310720

commit v2 on v1

--- a/solution.py
+++ b/solution.py
@@ -11,6 +11,8 @@
 HS = 64
 ONES = 16
 CHUNK = 256
+SUB = 128
+LAG = 6
 MESH = pl.DeviceIdType.MESH
 ANY = pl.BlockSpec(memory_space=pl.ANY)
 F32, BF16 = jnp.float32, jnp.bfloat16
@@ -66,6 +68,7 @@
     scores_b,
     staged,
     att,
+    gathered,
     middle,
     hidden,
     part_own,
@@ -82,24 +85,27 @@
 ):
     view, tok, obj = lax.axis_index("view"), lax.axis_index("tok"), lax.axis_index("obj")
     other, twin = 1 - tok, 1 - obj
-    rows = rows_in.shape[1]
     width = rows_in.shape[2]
+    rows = 2 * SUB
     half_of = (tok, other)
+    first, second = pl.ds(0, SUB), pl.ds(SUB, SUB)
+    sub = (first, second)
 
     def load(number, source, target):
         return pltpu.make_async_copy(source, target, load_sem.at[number])
 
     loads = [
-        load(0, latents, rows_in.at[0]),
-        load(1, key_weight, wk),
-        load(2, value_weight, wv),
-        load(3, query_weight, wq),
-        load(4, output_weight, wo.at[tok]),
-        load(5, value_units, vu),
-        load(6, gate_units, gu),
-        load(7, down_weight, dw),
+        load(0, latents.at[first], rows_in.at[0, first]),
+        load(1, latents.at[second], rows_in.at[0, second]),
+        load(2, key_weight, wk),
+        load(3, value_weight, wv),
+        load(4, query_weight, wq),
+        load(5, output_weight, wo.at[tok]),
+        load(6, value_units, vu),
+        load(7, gate_units, gu),
+        load(8, down_weight, dw),
     ]
-    for item in loads[:4]:
+    for item in loads[:5]:
         item.start()
 
     barrier = pltpu.get_barrier_semaphore()
@@ -120,159 +126,165 @@
             device_id_type=MESH,
         )
 
-    lat_copy = remote(rows_in.at[0], rows_in.at[1], lat_sem, (), {"tok": other})
-
-    loads[0].wait()
-    normed[...] = normalize(rows_in[0].astype(F32)).astype(BF16)
-    pl.semaphore_wait(barrier, views + 1)
-    lat_copy.start()
-
+    lat_copies = [
+        remote(rows_in.at[0, sub[ab]], rows_in.at[1, sub[ab]], lat_sem, (ab,), {"tok": other})
+        for ab in range(2)
+    ]
     far_first = sorted(range(1, views), key=lambda d: abs(d - views // 2))
 
-    def kv_copy(slot, d):
+    def kv_copy(chunk, d):
         peer = lax.rem(view + d, views)
         return remote(
-            send_kv.at[slot, peer], kv_all.at[slot, view], kv_sem, (slot, d), {"view": peer}
-        )
-
-    def q_copy(slot, d):
-        peer = lax.rem(view + d, views)
-        return remote(send_q.at[slot, peer], q_all.at[slot, view], q_sem, (slot, d), {"view": peer})
-
-    def kv_arrival(slot, d):
+            send_kv.at[chunk, peer], kv_all.at[chunk, view], kv_sem, (chunk, d), {"view": peer}
+        )
+
+    def q_copy(slot, ab, d):
+        peer, chunk = lax.rem(view + d, views), 2 * slot + ab
+        return remote(
+            send_q.at[chunk, peer],
+            q_all.at[ab, view, half_of[slot]],
+            q_sem,
+            (chunk, d),
+            {"view": peer},
+        )
+
+    def kv_arrival(chunk, d):
         source = lax.rem(view - d + views, views)
         return remote(
-            send_kv.at[slot, source], kv_all.at[slot, source], kv_sem, (slot, d), {"view": source}
-        )
-
-    def q_arrival(slot, d):
-        source = lax.rem(view - d + views, views)
+            send_kv.at[chunk, source], kv_all.at[chunk, source], kv_sem, (chunk, d), {"view": source}
+        )
+
+    def q_arrival(slot, ab, d):
+        source, chunk = lax.rem(view - d + views, views), 2 * slot + ab
         return remote(
-            send_q.at[slot, source], q_all.at[slot, source], q_sem, (slot, d), {"view": source}
-        )
-
-    def project(weight):
-        return jnp.dot(normed[...], weight[...], preferred_element_type=F32)
+            send_q.at[chunk, source],
+            q_all.at[ab, source, half_of[slot]],
+            q_sem,
+            (chunk, d),
+            {"view": source},
+        )
+
+    def level(slot, ab):
+        normed[2 * slot + ab] = normalize(rows_in[slot, sub[ab]].astype(F32)).astype(BF16)
+
+    def project(chunk, weight):
+        return jnp.dot(normed[chunk], weight[...], preferred_element_type=F32)
 
     def turned(projected):
-        return projected.astype(BF16).T.reshape(views, HS, rows)
-
-    def spread_kv(slot):
-        send_kv[slot, :, 0] = turned(project(wk))
-        send_kv[slot, :, 1] = turned(project(wv))
+        return projected.astype(BF16).T.reshape(views, HS, SUB)
+
+    def spread_kv(chunk):
+        send_kv[chunk, :, 0] = turned(project(chunk, wk))
+        send_kv[chunk, :, 1] = turned(project(chunk, wv))
         for d in far_first:
-            kv_copy(slot, d).start()
-        kv_all[slot, view] = send_kv[slot, view]
-
-    def spread_q(slot):
-        send_q[slot] = turned(project(wq) * (HS**-0.5 * math.log2(math.e)))
+            kv_copy(chunk, d).start()
+        kv_all[chunk, view] = send_kv[chunk, view]
+
+    def make_q(chunk):
+        send_q[chunk] = turned(project(chunk, wq) * (HS**-0.5 * math.log2(math.e)))
+
+    def spread_q(slot, ab):
         for d in far_first:
-            q_copy(slot, d).start()
-        q_all[slot, view] = send_q[slot, view]
-
+            q_copy(slot, ab, d).start()
+        q_all[ab, view, half_of[slot]] = send_q[2 * slot + ab, view]
+
+    loads[0].wait()
+    level(0, 0)
     loads[1].wait()
+    pl.semaphore_wait(barrier, views + 1)
+    for item in lat_copies:
+        item.start()
     loads[2].wait()
+    loads[3].wait()
     spread_kv(0)
-    loads[3].wait()
-    for item in loads[4:]:
+    level(0, 1)
+    spread_kv(1)
+    loads[4].wait()
+    for item in loads[5:]:
         item.start()
-    spread_q(0)
-
-    lat_copy.wait_recv()
-    loads[4].wait()
+    make_q(0)
+    make_q(1)
+
+    lat_copies[0].wait_recv()
+    level(1, 0)
+    spread_kv(2)
+    make_q(2)
+    lat_copies[1].wait_recv()
+    loads[5].wait()
     share = wo.shape[1] // 2
     mine, theirs = pl.ds(obj * share, share), pl.ds(twin * share, share)
     wo_across = remote(wo.at[tok, mine], wo.at[tok, mine], wo_sem, (0,), {"tok": other})
     wo_across.start()
-    normed[...] = normalize(rows_in[1].astype(F32)).astype(BF16)
-    spread_kv(1)
-    spread_q(1)
+    level(1, 1)
+    spread_kv(3)
+    spread_q(0, 0)
+    spread_q(1, 0)
+    make_q(3)
+    spread_q(0, 1)
+    spread_q(1, 1)
 
     vals[:, :, HS:, :] = jnp.ones((2, views, ONES, rows), BF16)
 
-    def prepare(slot):
+    def prepare(slot, ab):
+        chunk = 2 * slot + ab
+
         def one(d, carry):
             source = lax.rem(view - d + views, views)
 
             @pl.when(d > 0)
             def _():
-                kv_arrival(slot, d).wait_recv()
-
-            keys[slot, source] = kv_all[slot, source, 0].T
-            vals[slot, source, :HS, :] = kv_all[slot, source, 1]
+                kv_arrival(chunk, d).wait_recv()
+
+            keys[slot, source, sub[ab]] = kv_all[chunk, source, 0].T
+            vals[slot, source, :HS, sub[ab]] = kv_all[chunk, source, 1]
             return carry
 
         lax.fori_loop(0, views, one, 0)
 
-    prepare(0)
-    prepare(1)
+    for chunk in range(4):
+        prepare(chunk // 2, chunk % 2)
 
     steps = 2 * views
     blocks = [(slot, number) for slot in range(2) for number in range(views)]
 
     def place(n):
-        slot, turn = n // views, lax.rem(n, views) + 1
-        return slot, turn, lax.rem(view + turn, views)
+        ab, turn = n // views, lax.rem(n, views) + 1
+        return ab, turn, lax.rem(view + turn, views), lax.rem(view - turn + views, views)
 
     def fetch_q(n):
-        slot, turn, target = place(n)
+        ab, turn, target, _ = place(n)
 
         @pl.when(turn != views)
         def _():
-            q_arrival(slot, views - turn).wait_recv()
+            for slot in range(2):
+                q_arrival(slot, ab, views - turn).wait_recv()
 
     def att_copy(n):
-        slot, turn, target = place(n)
-        half = jnp.where(slot == 0, tok, other)
+        ab, turn, target, _ = place(n)
         return remote(
-            staged.at[slot, target],
-            att.at[half, tok, view],
-            att_sem,
-            (slot, turn),
-            {"view": target},
+            staged.at[ab, target], att.at[ab, tok, view], att_sem, (ab, turn), {"view": target}
         )
 
     def att_arrival(n):
-        slot, turn, _ = place(n)
-        half = jnp.where(slot == 0, tok, other)
-        source = lax.rem(view - turn + views, views)
+        ab, turn, _, source = place(n)
         return remote(
-            staged.at[slot, source],
-            att.at[half, tok, source],
-            att_sem,
-            (slot, turn),
-            {"view": source},
+            staged.at[ab, source], att.at[ab, tok, source], att_sem, (ab, turn), {"view": source}
         )
 
     def relay_copy(n):
-        slot, turn, _ = place(n)
-        half = jnp.where(slot == 0, tok, other)
-        source = lax.rem(view - turn + views, views)
-        return remote(
-            att.at[half, tok, source],
-            att.at[half, tok, source],
-            relay_sem,
-            (slot, turn),
-            {"tok": other},
-        )
+        ab, turn, _, source = place(n)
+        block = att.at[ab, tok, source]
+        return remote(block, block, relay_sem, (ab, turn), {"tok": other})
 
     def relay_arrival(n):
-        slot, turn, _ = place(n)
-        half = jnp.where(slot == 0, other, tok)
-        source = lax.rem(view - turn + views, views)
-        return remote(
-            att.at[half, other, source],
-            att.at[half, other, source],
-            relay_sem,
-            (slot, turn),
-            {"tok": other},
-        )
+        ab, turn, _, source = place(n)
+        block = att.at[ab, other, source]
+        return remote(block, block, relay_sem, (ab, turn), {"tok": other})
 
     def score(n, buffer, number):
-        slot, turn, target = place(n)
-        found = jnp.dot(
-            keys[blocks[number]], q_all[slot, target], preferred_element_type=F32
-        )
+        ab, _, target, _ = place(n)
+        queries = jnp.concatenate([q_all[ab, target, 0], q_all[ab, target, 1]], 1)
+        found = jnp.dot(keys[blocks[number]], queries, preferred_element_type=F32)
         buffer[number] = found
         return jnp.max(found, 0, keepdims=True)
 
@@ -288,13 +300,13 @@
                 upcoming = jnp.maximum(upcoming, score(n + 1, following, number))
             blended = blended + blend(current, highest, number)
         result = (blended[:HS] / blended[HS : HS + 1]).astype(BF16)
-        slot, turn, target = place(n)
-        staged[slot, target] = result
+        ab, _, target, _ = place(n)
+        staged[ab, target, 0] = result[:, :SUB]
+        staged[ab, target, 1] = result[:, SUB:]
         return upcoming
 
     def post(n):
-        slot, turn, target = place(n)
-        half = jnp.where(slot == 0, tok, other)
+        ab, turn, target, _ = place(n)
 
         @pl.when(turn != views)
         def _():
@@ -302,10 +314,10 @@
 
         @pl.when(turn == views)
         def _():
-            att[half, tok, view] = staged[slot, view]
+            att[ab, tok, view] = staged[ab, view]
 
     def relay(n):
-        slot, turn, target = place(n)
+        _, turn, _, _ = place(n)
 
         @pl.when(turn != views)
         def _():
@@ -320,8 +332,6 @@
             highest = jnp.maximum(highest, score(0, scores_a, number))
         return highest
 
-    LAG = 2
-
     def two_steps(i, highest):
         n = 2 * i
         fetch_q(n + 1)
@@ -348,100 +358,97 @@
     fetch_q(last + 1)
     highest = unit(last, scores_a, highest, scores_b)
     post(last)
-    relay(last - LAG)
     wo_arrival = remote(wo.at[other, mine], wo.at[other, mine], wo_sem, (0,), {"tok": other})
     wo_arrival.wait_recv()
     wo_swap = remote(wo.at[other, mine], wo.at[other, mine], wo_sem, (1,), {"obj": twin})
     wo_swap.start()
     unit(last + 1, scores_b, highest, None)
     post(last + 1)
-    relay(last + 1 - LAG)
-    relay(last)
-    relay(last + 1)
+
+    def relay_rest(n, carry):
+        relay(n)
+        return carry
+
+    lax.fori_loop(last - LAG, steps, relay_rest, 0)
 
     remote(wo.at[other, theirs], wo.at[other, theirs], wo_sem, (1,), {"obj": twin}).wait_recv()
 
     columns = width // CHUNK
 
-    def join(slot):
-        half = half_of[slot]
-        gathered = att[half].reshape(2 * views * HS, rows).T
-
-        def one(c, carry):
-            at = pl.ds(pl.multiple_of(c * CHUNK, CHUNK), CHUNK)
+    def join(slot, ab):
+        at_rows = pl.ds(pl.multiple_of(ab * SUB, SUB), SUB)
+        gathered[...] = att[ab, :, :, half_of[slot]].reshape(2 * views * HS, SUB).T
+        for c in range(columns):
+            at = slice(c * CHUNK, (c + 1) * CHUNK)
             whole = wo[:, :, at].reshape(2 * views * HS, CHUNK)
-            middle[slot, :, at] = rows_in[slot, :, at].astype(F32) + jnp.dot(
-                gathered, whole, preferred_element_type=F32
+            middle[slot, at_rows, at] = rows_in[slot, at_rows, at].astype(F32) + jnp.dot(
+                gathered[...], whole, preferred_element_type=F32
             )
-            return carry
-
-        lax.fori_loop(0, columns, one, 0)
-        normed[...] = normalize(middle[slot]).astype(BF16)
-
-    def units():
+        normed[2 * slot + ab] = normalize(middle[slot, at_rows]).astype(BF16)
+
+    def units(block, target):
         wide = 2 * CHUNK
-
-        def one(c, carry):
-            at = pl.ds(pl.multiple_of(c * wide, wide), wide)
-            block = normed[...]
+        for c in range(hidden.shape[1] // wide):
+            at = slice(c * wide, (c + 1) * wide)
             linear = jnp.dot(block, vu[:, at], preferred_element_type=F32)
             gating = jnp.dot(block, gu[:, at], preferred_element_type=F32)
-            hidden[:, at] = (linear * gelu(gating)).astype(BF16)
+            target[:, at] = (linear * gelu(gating)).astype(BF16)
+
+    def part_copy(ab, c):
+        return remote(part_out.at[ab, c], part_in.at[ab, c], part_sem, (ab, c), {"tok": other})
+
+    def for_partner(ab, carry):
+        def one(n, carry):
+            relay_arrival(ab * views + n).wait_recv()
             return carry
 
-        lax.fori_loop(0, hidden.shape[1] // wide, one, 0)
-
-    def down(c):
+        lax.fori_loop(0, views, one, 0)
+        join(1, ab)
+        units(normed[2 + ab], hidden.at[first])
+        for c in range(columns):
+            at = slice(c * CHUNK, (c + 1) * CHUNK)
+            part = jnp.dot(hidden[first], dw[:, at], preferred_element_type=F32)
+            part_out[ab, c] = part.astype(BF16)
+            part_copy(ab, c).start()
+        return carry
+
+    for item in loads[6:]:
+        item.wait()
+    lax.fori_loop(0, 2, for_partner, 0)
+
+    def join_own(ab, carry):
+        join(0, ab)
+        return carry
+
+    lax.fori_loop(0, 2, join_own, 0)
+    units(normed[:2].reshape(rows, width), hidden)
+
+    def keep_part(c, carry):
         at = pl.ds(pl.multiple_of(c * CHUNK, CHUNK), CHUNK)
-        return jnp.dot(hidden[...], dw[:, at], preferred_element_type=F32)
-
-    def part_copy(c):
-        return remote(part_out.at[c], part_in.at[c], part_sem, (c,), {"tok": other})
-
-    def wait_relays(first):
-        def one(n, carry):
-            relay_arrival(first + n).wait_recv()
-            return carry
-
-        lax.fori_loop(0, views, one, 0)
-
-    wait_relays(0)
-    join(1)
-    for item in loads[5:]:
-        item.wait()
-    units()
-
-    def send_part(c, carry):
-        part_out[c] = down(c).astype(BF16)
-        part_copy(c).start()
+        part_own[c] = jnp.dot(hidden[...], dw[:, at], preferred_element_type=F32)
         return carry
 
-    lax.fori_loop(0, columns, send_part, 0)
-    wait_relays(views)
-    join(0)
-    units()
-
-    def keep_part(c, carry):
-        part_own[c] = down(c)
-        return carry
-
     lax.fori_loop(0, columns, keep_part, 0)
 
-    for c in range(columns):
-        part_copy(c).wait_recv()
-        at = slice(c * CHUNK, (c + 1) * CHUNK)
-        total = middle[0, :, at] + part_own[c] + part_in[c].astype(F32)
-        out_ref[:, at] = total.astype(BF16)
-
-    lat_copy.wait_send()
+    for ab in range(2):
+        for c in range(columns):
+            part_copy(ab, c).wait_recv()
+            at = slice(c * CHUNK, (c + 1) * CHUNK)
+            total = middle[0, sub[ab], at] + part_own[c, sub[ab]] + part_in[ab, c].astype(F32)
+            out_ref[sub[ab], at] = total.astype(BF16)
+
+    for item in lat_copies:
+        item.wait_send()
     wo_across.wait_send()
     wo_swap.wait_send()
 
     def drain(d, carry):
         for slot in range(2):
-            kv_copy(slot, d).wait_send()
-            q_copy(slot, d).wait_send()
-            att_copy(slot * views + d - 1).wait_send()
+            for ab in range(2):
+                kv_copy(2 * slot + ab, d).wait_send()
+                q_copy(slot, ab, d).wait_send()
+        for ab in range(2):
+            att_copy(ab * views + d - 1).wait_send()
         return carry
 
     lax.fori_loop(1, views, drain, 0)
@@ -453,7 +460,8 @@
     lax.fori_loop(0, steps, drain_relays, 0)
 
     def drain_parts(c, carry):
-        part_copy(c).wait_send()
+        for ab in range(2):
+            part_copy(ab, c).wait_send()
         return carry
 
     lax.fori_loop(0, columns, drain_parts, 0)
@@ -466,7 +474,6 @@
     rows = stream.shape[0]
     head_width, units = weights[0].shape[1], weights[4].shape[1]
     columns = width // CHUNK
-    half = (2, views)
     dma = pltpu.SemaphoreType.DMA
     scratch = [
         pltpu.VMEM((2, rows, width), BF16),
@@ -477,30 +484,31 @@
         pltpu.VMEM((width, units), BF16),
         pltpu.VMEM((width, units), BF16),
         pltpu.VMEM((units, width), BF16),
-        pltpu.VMEM((rows, width), BF16),
-        pltpu.VMEM(half + (HS, rows), BF16),
-        pltpu.VMEM(half + (2, HS, rows), BF16),
-        pltpu.VMEM(half + (HS, rows), BF16),
-        pltpu.VMEM(half + (2, HS, rows), BF16),
-        pltpu.VMEM(half + (rows, HS), BF16),
-        pltpu.VMEM(half + (HS + ONES, rows), BF16),
+        pltpu.VMEM((4, SUB, width), BF16),
+        pltpu.VMEM((4, views, HS, SUB), BF16),
+        pltpu.VMEM((4, views, 2, HS, SUB), BF16),
+        pltpu.VMEM((2, views, 2, HS, SUB), BF16),
+        pltpu.VMEM((4, views, 2, HS, SUB), BF16),
+        pltpu.VMEM((2, views, rows, HS), BF16),
+        pltpu.VMEM((2, views, HS + ONES, rows), BF16),
         pltpu.VMEM((2 * views, rows, rows), F32),
         pltpu.VMEM((2 * views, rows, rows), F32),
-        pltpu.VMEM(half + (HS, rows), BF16),
-        pltpu.VMEM((2, 2, views, HS, rows), BF16),
+        pltpu.VMEM((2, views, 2, HS, SUB), BF16),
+        pltpu.VMEM((2, 2, views, 2, HS, SUB), BF16),
+        pltpu.VMEM((SUB, 2 * head_width), BF16),
         pltpu.VMEM((2, rows, width), F32),
         pltpu.VMEM((rows, units), BF16),
         pltpu.VMEM((columns, rows, CHUNK), F32),
-        pltpu.VMEM((columns, rows, CHUNK), BF16),
-        pltpu.VMEM((columns, rows, CHUNK), BF16),
-        dma((8,)),
-        dma((2,)),
-        dma((2, 2, views)),
-        dma((2, 2, views)),
+        pltpu.VMEM((2, columns, SUB, CHUNK), BF16),
+        pltpu.VMEM((2, columns, SUB, CHUNK), BF16),
+        dma((9,)),
+        dma((2, 2)),
+        dma((2, 4, views)),
+        dma((2, 4, views)),
         dma((2, 2)),
         dma((2, 2, views + 1)),
         dma((2, 2, views + 1)),
-        dma((2, columns)),
+        dma((2, 2, columns)),
     ]
     result = pl.pallas_call(
         functools.partial(block_kernel, views),
@@ -509,7 +517,7 @@
         out_specs=pl.BlockSpec(memory_space=pltpu.VMEM),
         scratch_shapes=scratch,
         compiler_params=pltpu.CompilerParams(
-            collective_id=0, has_side_effects=True, vmem_limit_bytes=62 * 1024 * 1024
+            collective_id=0, has_side_effects=True, vmem_limit_bytes=56 * 1024 * 1024
         ),
         name="block",
     )(stream, *weights)
@@ -628,7 +636,7 @@
         and head_width == lax.axis_size("view") * HS
         and lax.axis_size("tok") == 2
         and lax.axis_size("obj") == 2
-        and rows == CHUNK
+        and rows == 2 * SUB
         and width % CHUNK == 0
         and unit_width % (2 * CHUNK) == 0
     )

time: 92.7 us -> 81.1 us (0.87)
  Pallas kernels: 90.6 us -> 78.9 us
    pallas_call x1, Pallas kernels: 90.6 us -> 78.9 us  [by_heads(): pl.pallas_call(functools.partial(block_kernel, views), out_shape=jax.Shap...]
where the time goes in v2:
time: 81.1 us; the launch traced here: 80.9 us
  Pallas kernels  78.9 us (97%)
  local copies, waits for them, and re-layouts  1.97 us (2%)
    pallas_call x1, Pallas kernels, by_heads(): pl.pallas_call(functools.partial(block_kernel, views), out_shape=jax.Shap...  78.9 us
    unnamed x1, local copies, waits for them, and re-layouts  1.97 us

profile of v2, /device:TPU:0, one launch (start us, length us, event | category | flops | bytes accessed | tf_op | source)
XLA Modules:
  0.0 80.9 jit_solution(11701719869906277549)
XLA Ops:
  0.0 78.9 %block.1 = bf16[256,1280]{1,0:T(8,128)(2,1)} custom-call(bf16[256,1280]{1,0:T(8,128)(2,1)} %bitcast.3, bf16[1280,512]{1,0:T(8,128)(2,1)} %query_weight.1, bf16[1280,512]{1,0:T(8,128)(2,1)} %key_weight.1, bf16[1280,512]{1,0:T(8,128)(2,1)} %value_weight.1, bf16[512,1280]{1,0:T(8,128)(2,1)} %output_weight.1, bf16[1280,2560]{1,0:T(8,128)(2,1)} %value_units.1, ...), custom_call_target="tpu_custom_call" | custom-call | tf_op jit(solution)/shard_map/block/pallas_call | solution.py:513
  78.9 2.0 %copy.10 = bf16[256,1,1,1280]{3,0,2,1:T(8,128)(2,1)} copy(bf16[256,1,1,1280]{3,0,2,1:T(8,128)(2,1)} %bitcast.2) | data formatting | bytes 1310720

commit v3 on v2

--- a/solution.py
+++ b/solution.py
@@ -12,7 +12,7 @@
 ONES = 16
 CHUNK = 256
 SUB = 128
-LAG = 6
+LAG = 5
 MESH = pl.DeviceIdType.MESH
 ANY = pl.BlockSpec(memory_space=pl.ANY)
 F32, BF16 = jnp.float32, jnp.bfloat16
@@ -184,7 +184,7 @@
         send_q[chunk] = turned(project(chunk, wq) * (HS**-0.5 * math.log2(math.e)))
 
     def spread_q(slot, ab):
-        for d in far_first:
+        for d in range(views - 1, 0, -1):
             q_copy(slot, ab, d).start()
         q_all[ab, view, half_of[slot]] = send_q[2 * slot + ab, view]
 
@@ -217,11 +217,7 @@
     wo_across.start()
     level(1, 1)
     spread_kv(3)
-    spread_q(0, 0)
-    spread_q(1, 0)
     make_q(3)
-    spread_q(0, 1)
-    spread_q(1, 1)
 
     vals[:, :, HS:, :] = jnp.ones((2, views, ONES, rows), BF16)
 
@@ -241,14 +237,34 @@
 
         lax.fori_loop(0, views, one, 0)
 
-    for chunk in range(4):
+    for chunk in range(3):
         prepare(chunk // 2, chunk % 2)
+
+    def left(d, carry):
+        kv_copy(3, d).wait_send()
+        return carry
+
+    lax.fori_loop(1, views, left, 0)
+    spread_q(0, 0)
+    spread_q(1, 0)
+    prepare(1, 1)
+
+    def left_too(d, carry):
+        for slot in range(2):
+            q_copy(slot, 0, d).wait_send()
+        return carry
+
+    lax.fori_loop(1, views, left_too, 0)
+    spread_q(0, 1)
+    spread_q(1, 1)
 
     steps = 2 * views
     blocks = [(slot, number) for slot in range(2) for number in range(views)]
 
     def place(n):
-        ab, turn = n // views, lax.rem(n, views) + 1
+        later = n - 2
+        ab = jnp.where(later < 0, n, later // (views - 1))
+        turn = jnp.where(later < 0, views, lax.rem(later + views - 1, views - 1) + 1)
         return ab, turn, lax.rem(view + turn, views), lax.rem(view - turn + views, views)
 
     def fetch_q(n):
@@ -259,8 +275,8 @@
             for slot in range(2):
                 q_arrival(slot, ab, views - turn).wait_recv()
 
-    def att_copy(n):
-        ab, turn, target, _ = place(n)
+    def att_copy(ab, turn):
+        target = lax.rem(view + turn, views)
         return remote(
             staged.at[ab, target], att.at[ab, tok, view], att_sem, (ab, turn), {"view": target}
         )
@@ -271,13 +287,13 @@
             staged.at[ab, source], att.at[ab, tok, source], att_sem, (ab, turn), {"view": source}
         )
 
-    def relay_copy(n):
-        ab, turn, _, source = place(n)
+    def relay_copy(ab, turn):
+        source = lax.rem(view - turn + views, views)
         block = att.at[ab, tok, source]
         return remote(block, block, relay_sem, (ab, turn), {"tok": other})
 
-    def relay_arrival(n):
-        ab, turn, _, source = place(n)
+    def relay_arrival(ab, turn):
+        source = lax.rem(view - turn + views, views)
         block = att.at[ab, other, source]
         return remote(block, block, relay_sem, (ab, turn), {"tok": other})
 
@@ -310,20 +326,20 @@
 
         @pl.when(turn != views)
         def _():
-            att_copy(n).start()
+            att_copy(ab, turn).start()
 
         @pl.when(turn == views)
         def _():
             att[ab, tok, view] = staged[ab, view]
 
     def relay(n):
-        _, turn, _, _ = place(n)
+        ab, turn, _, _ = place(n)
 
         @pl.when(turn != views)
         def _():
             att_arrival(n).wait_recv()
 
-        relay_copy(n).start()
+        relay_copy(ab, turn).start()
 
     def first_scores():
         fetch_q(0)
@@ -332,8 +348,17 @@
             highest = jnp.maximum(highest, score(0, scores_a, number))
         return highest
 
+    wo_arrival = remote(wo.at[other, mine], wo.at[other, mine], wo_sem, (0,), {"tok": other})
+    wo_swap = remote(wo.at[other, mine], wo.at[other, mine], wo_sem, (1,), {"obj": twin})
+
     def two_steps(i, highest):
         n = 2 * i
+
+        @pl.when(i == views // 2)
+        def _():
+            wo_arrival.wait_recv()
+            wo_swap.start()
+
         fetch_q(n + 1)
         highest = unit(n, scores_a, highest, scores_b)
         post(n)
@@ -351,6 +376,13 @@
             relay(n + 1 - LAG)
 
         return highest
+
+    def relays(start, stop):
+        def one(n, carry):
+            relay(n)
+            return carry
+
+        lax.fori_loop(start, stop, one, 0)
 
     highest = first_scores()
     highest = lax.fori_loop(0, views - 1, two_steps, highest)
@@ -358,20 +390,10 @@
     fetch_q(last + 1)
     highest = unit(last, scores_a, highest, scores_b)
     post(last)
-    wo_arrival = remote(wo.at[other, mine], wo.at[other, mine], wo_sem, (0,), {"tok": other})
-    wo_arrival.wait_recv()
-    wo_swap = remote(wo.at[other, mine], wo.at[other, mine], wo_sem, (1,), {"obj": twin})
-    wo_swap.start()
+    relay(last - LAG)
     unit(last + 1, scores_b, highest, None)
     post(last + 1)
-
-    def relay_rest(n, carry):
-        relay(n)
-        return carry
-
-    lax.fori_loop(last - LAG, steps, relay_rest, 0)
-
-    remote(wo.at[other, theirs], wo.at[other, theirs], wo_sem, (1,), {"obj": twin}).wait_recv()
+    relay(last + 1 - LAG)
 
     columns = width // CHUNK
 
@@ -397,44 +419,49 @@
     def part_copy(ab, c):
         return remote(part_out.at[ab, c], part_in.at[ab, c], part_sem, (ab, c), {"tok": other})
 
-    def for_partner(ab, carry):
+    def relayed(ab):
         def one(n, carry):
-            relay_arrival(ab * views + n).wait_recv()
+            relay_arrival(ab, n).wait_recv()
             return carry
 
-        lax.fori_loop(0, views, one, 0)
-        join(1, ab)
-        units(normed[2 + ab], hidden.at[first])
+        lax.fori_loop(1, views + 1, one, 0)
+
+    def down(c):
+        at = slice(c * CHUNK, (c + 1) * CHUNK)
+        return jnp.dot(hidden[...], dw[:, at], preferred_element_type=F32)
+
+    def send_parts(ab):
         for c in range(columns):
-            at = slice(c * CHUNK, (c + 1) * CHUNK)
-            part = jnp.dot(hidden[first], dw[:, at], preferred_element_type=F32)
-            part_out[ab, c] = part.astype(BF16)
+            part_out[ab, c] = down(c).astype(BF16)
+        for c in range(columns):
             part_copy(ab, c).start()
-        return carry
+
+    def keep_parts(ab):
+        for c in range(columns):
+            part_own[ab, c] = down(c)
 
     for item in loads[6:]:
         item.wait()
-    lax.fori_loop(0, 2, for_partner, 0)
-
-    def join_own(ab, carry):
+    remote(wo.at[other, theirs], wo.at[other, theirs], wo_sem, (1,), {"obj": twin}).wait_recv()
+    relayed(0)
+    join(1, 0)
+    relays(2 * views - LAG, 2 * views)
+    units(normed[2], hidden)
+    send_parts(0)
+    relayed(1)
+    join(1, 1)
+    units(normed[3], hidden)
+    send_parts(1)
+    for ab in range(2):
         join(0, ab)
-        return carry
-
-    lax.fori_loop(0, 2, join_own, 0)
-    units(normed[:2].reshape(rows, width), hidden)
-
-    def keep_part(c, carry):
-        at = pl.ds(pl.multiple_of(c * CHUNK, CHUNK), CHUNK)
-        part_own[c] = jnp.dot(hidden[...], dw[:, at], preferred_element_type=F32)
-        return carry
-
-    lax.fori_loop(0, columns, keep_part, 0)
+        units(normed[ab], hidden)
+        keep_parts(ab)
 
     for ab in range(2):
         for c in range(columns):
             part_copy(ab, c).wait_recv()
             at = slice(c * CHUNK, (c + 1) * CHUNK)
-            total = middle[0, sub[ab], at] + part_own[c, sub[ab]] + part_in[ab, c].astype(F32)
+            total = middle[0, sub[ab], at] + part_own[ab, c] + part_in[ab, c].astype(F32)
             out_ref[sub[ab], at] = total.astype(BF16)
 
     for item in lat_copies:
@@ -445,19 +472,21 @@
     def drain(d, carry):
         for slot in range(2):
             for ab in range(2):
-                kv_copy(2 * slot + ab, d).wait_send()
-                q_copy(slot, ab, d).wait_send()
+                if 2 * slot + ab < 3:
+                    kv_copy(2 * slot + ab, d).wait_send()
+            q_copy(slot, 1, d).wait_send()
         for ab in range(2):
-            att_copy(ab * views + d - 1).wait_send()
+            att_copy(ab, d).wait_send()
         return carry
 
     lax.fori_loop(1, views, drain, 0)
 
     def drain_relays(n, carry):
-        relay_copy(n).wait_send()
+        for ab in range(2):
+            relay_copy(ab, n).wait_send()
         return carry
 
-    lax.fori_loop(0, steps, drain_relays, 0)
+    lax.fori_loop(1, views + 1, drain_relays, 0)
 
     def drain_parts(c, carry):
         for ab in range(2):
@@ -497,8 +526,8 @@
         pltpu.VMEM((2, 2, views, 2, HS, SUB), BF16),
         pltpu.VMEM((SUB, 2 * head_width), BF16),
         pltpu.VMEM((2, rows, width), F32),
-        pltpu.VMEM((rows, units), BF16),
-        pltpu.VMEM((columns, rows, CHUNK), F32),
+        pltpu.VMEM((SUB, units), BF16),
+        pltpu.VMEM((2, columns, SUB, CHUNK), F32),
         pltpu.VMEM((2, columns, SUB, CHUNK), BF16),
         pltpu.VMEM((2, columns, SUB, CHUNK), BF16),
         dma((9,)),

time: 81.1 us -> 80 us (0.986)
  Pallas kernels: 78.9 us -> 77.8 us
    pallas_call x1, Pallas kernels: 78.9 us -> 77.8 us  [by_heads(): pl.pallas_call(functools.partial(block_kernel, views), out_shape=jax.Shap...]
where the time goes in v3:
time: 80 us; the launch traced here: 79.8 us
  Pallas kernels  77.8 us (97%)
  local copies, waits for them, and re-layouts  1.97 us (2%)
    pallas_call x1, Pallas kernels, by_heads(): pl.pallas_call(functools.partial(block_kernel, views), out_shape=jax.Shap...  77.8 us
    unnamed x1, local copies, waits for them, and re-layouts  1.97 us

profile of v3, /device:TPU:0, one launch (start us, length us, event | category | flops | bytes accessed | tf_op | source)
XLA Modules:
  0.0 79.8 jit_solution(11815713358458621066)
XLA Ops:
  0.0 77.8 %block.1 = bf16[256,1280]{1,0:T(8,128)(2,1)} custom-call(bf16[256,1280]{1,0:T(8,128)(2,1)} %bitcast.3, bf16[1280,512]{1,0:T(8,128)(2,1)} %query_weight.1, bf16[1280,512]{1,0:T(8,128)(2,1)} %key_weight.1, bf16[1280,512]{1,0:T(8,128)(2,1)} %value_weight.1, bf16[512,1280]{1,0:T(8,128)(2,1)} %output_weight.1, bf16[1280,2560]{1,0:T(8,128)(2,1)} %value_units.1, ...), custom_call_target="tpu_custom_call" | custom-call | tf_op jit(solution)/shard_map/block/pallas_call | solution.py:542
  77.9 2.0 %copy.10 = bf16[256,1,1,1280]{3,0,2,1:T(8,128)(2,1)} copy(bf16[256,1,1,1280]{3,0,2,1:T(8,128)(2,1)} %bitcast.2) | data formatting | bytes 1310720
